TPU v7x, 32 devices: a whole 2x2x4 slice. The times are simulated.
32 devices in a mesh: seq: 4 (over z), grp: 8 (over y, x, core).
Axes of the slice: x: 2, y: 2, z: 4, core: 2. Of those that a mesh axis runs over, the one named last changes fastest.
Arguments:
- hidden_in: bfloat16 [8, 2048, 1024], P('grp', 'seq'), may hold values from -64 to 64, as said below
- lengths: int32 [8], P('grp'), may hold values from 256 to 2048
- project_weight: bfloat16 [1024, 3072], replicated, may hold values from -0.1875 to 0.1875
- output_weight: bfloat16 [1024, 1024], replicated, may hold values from -0.1875 to 0.1875
- first_gain: float32 [1024], replicated, may hold values from 0.5 to 1.5
- first_shift: float32 [1024], replicated, may hold values from -3 to 3
- up_weight: bfloat16 [1024, 4096], P('grp'), may hold values from -0.1875 to 0.1875
- down_weight: bfloat16 [1024, 4096], P('grp'), may hold values from -0.09375 to 0.09375
- second_gain: float32 [1024], replicated, may hold values from 0.5 to 1.5
- second_shift: float32 [1024], replicated, may hold values from -3 to 3
- queries: float32 [64, 1024], P('grp'), may hold values from -6 to 6
- positive: int32 [64], P('grp'), may hold values from 0 to 7
Outputs:
- hidden_out: bfloat16 [8, 2048, 1024], P('grp', 'seq')
- embeddings: float32 [8, 1024], P('grp')
- query_loss: float32 [64], P('grp')
Inputs may be any that keep to these rules, and one draw needn't show every extreme that they name: `hidden_in`: activations.
All inputs are finite; a program needn't handle non-finite values.
Results may differ from a plain program's by a relative error of at most 0.0076.
Values may be sent and summed in bfloat16 or wider, within the bound.
A program may use at most 192 MiB of HBM per device.

v0:
```python
import functools
import math

import jax
import jax.numpy as jnp
from jax import lax
from jax.experimental import pallas as pl
from jax.experimental.pallas import tpu as pltpu
from jax.sharding import PartitionSpec as P

HEAD_DIM = 64
PAIR = 2 * HEAD_DIM
LOW = -1e30
TILE = 256
HALVES = 2
MESH = pl.DeviceIdType.MESH
F32 = jnp.float32
BF16 = jnp.bfloat16


def layer_norm(values, gain, shift):
    average = jnp.mean(values, axis=-1, keepdims=True)
    centred = values - average
    variance = jnp.mean(centred * centred, axis=-1, keepdims=True)
    return centred * lax.rsqrt(variance + 1e-05) * gain + shift


def span(index, size):
    return pl.ds(pl.multiple_of(index * size, size), size)


def flip(index, bit):
    step = 1 << bit
    return index + (1 - 2 * ((index // step) % 2)) * step


class Gather:
    def __init__(self, source, held, send, recv, mine, order):
        self.source, self.held, self.send_sem, self.recv_sem = source, held, send, recv
        self.mine, self.order = mine, order
        self.rows = source.shape[0]

    def origin(self, piece, base):
        for place, bit in enumerate(self.order):
            if (piece >> place) & 1:
                base = flip(base, bit)
        return base

    def copy(self, stage, piece, incoming):
        peer = flip(self.mine, self.order[stage])
        owner = self.origin(piece, peer if incoming else self.mine)
        there = self.held.at[span(owner, self.rows)]
        slot = (1 << stage) - 1 + piece
        return pltpu.make_async_remote_copy(
            src_ref=self.source if piece == 0 and not incoming else there,
            dst_ref=there,
            send_sem=self.send_sem.at[slot],
            recv_sem=self.recv_sem.at[slot],
            device_id={"grp": peer},
            device_id_type=MESH,
        )

    def begin(self, stage):
        self.copy(stage, 0, False).start()

    def pass_on(self, stage, piece):
        self.copy(stage, piece, True).wait_recv()
        for later in range(stage + 1, len(self.order)):
            self.copy(later, (1 << stage) + piece, False).start()

    def drain(self):
        for stage in range(len(self.order)):
            for piece in range(1 << stage):
                self.copy(stage, piece, False).wait_send()


def kernel(
    seq_size,
    grp_size,
    tok_hbm,
    length_ref,
    wp_hbm,
    wo_hbm,
    gain1,
    shift1,
    up_hbm,
    down_hbm,
    gain2,
    shift2,
    query_ref,
    positive_ref,
    out_hbm,
    emb_out,
    loss_out,
    hid,
    wp,
    wo,
    up,
    down,
    qm,
    kbuf,
    vt,
    acc,
    high,
    summed,
    bias,
    att,
    normed,
    inner,
    outer,
    final,
    totals,
    embeds,
    local_sem,
    below_send,
    below_recv,
    above_send,
    above_recv,
    up_send,
    up_recv,
    down_send,
    down_recv,
    tot_send,
    tot_recv,
    emb_send,
    emb_recv,
):
    rank = lax.axis_index("seq")
    group = lax.axis_index("grp")
    rows, width = tok_hbm.shape[1:]
    ff = up_hbm.shape[1]
    heads = width // HEAD_DIM
    pairs = width // PAIR
    part = rows // HALVES
    length = length_ref[0]
    bits = grp_size.bit_length() - 1

    barrier = pltpu.get_barrier_semaphore()
    for step in range(1, seq_size):
        pl.semaphore_signal(
            barrier,
            inc=1,
            device_id={"seq": (rank + step) % seq_size},
            device_id_type=MESH,
        )
    for step in range(1, grp_size):
        pl.semaphore_signal(
            barrier,
            inc=1,
            device_id={"grp": (group + step) % grp_size},
            device_id_type=MESH,
        )
    loads = [
        pltpu.make_async_copy(tok_hbm.at[0], hid.at[span(rank, rows)], local_sem.at[0]),
        pltpu.make_async_copy(wp_hbm, wp, local_sem.at[1]),
        pltpu.make_async_copy(wo_hbm, wo, local_sem.at[2]),
        pltpu.make_async_copy(up_hbm, up.at[span(group, up_hbm.shape[0])], local_sem.at[3]),
        pltpu.make_async_copy(down_hbm, down.at[span(group, down_hbm.shape[0])], local_sem.at[4]),
    ]
    for load in loads:
        load.start()
    pl.semaphore_wait(barrier, seq_size - 1 + grp_size - 1)

    def chain(upward, step, half, incoming, first=False):
        way = 1 if upward else -1
        owner = rank - way * step if incoming else rank - way * (step - 1)
        there = hid.at[span(owner * HALVES + half, part)]
        slot = (step - 1) * HALVES + half
        sends, recvs = (below_send, below_recv) if upward else (above_send, above_recv)
        return pltpu.make_async_remote_copy(
            src_ref=tok_hbm.at[0, pl.ds(half * part, part)] if first else there,
            dst_ref=there,
            send_sem=sends.at[slot],
            recv_sem=recvs.at[slot],
            device_id={"seq": rank + way},
            device_id_type=MESH,
        )

    def has_next(upward):
        return rank + 1 < seq_size if upward else rank >= 1

    def holds(upward, step):
        return rank - step >= 0 if upward else rank + step < seq_size

    for half in range(HALVES):
        for upward in (True, False):

            @pl.when(has_next(upward))
            def _(upward=upward, half=half):
                chain(upward, 1, half, False, True).start()

    order = list(range(1, bits)) + [0]
    back = list(reversed(range(1, bits))) + [0]
    ups = Gather(up_hbm, up, up_send, up_recv, group, order)
    downs = Gather(down_hbm, down, down_send, down_recv, group, back)
    for stage in range(bits):
        ups.begin(stage)
        downs.begin(stage)
    events = [(stage, piece) for stage in range(bits - 1) for piece in range(1 << stage)]

    loads[0].wait()
    loads[1].wait()

    lane = lax.broadcasted_iota(jnp.int32, (1, PAIR), 1)
    left = jnp.where(lane < HEAD_DIM, 1.0, 0.0).astype(BF16)
    right = jnp.where(lane < HEAD_DIM, 0.0, 1.0).astype(BF16)
    factor = math.log2(math.e) / math.sqrt(HEAD_DIM)
    own = span(rank, rows)

    @pl.loop(0, width // TILE)
    def _(tile):
        query = jnp.dot(hid[own, :], wp[:, span(tile, TILE)], preferred_element_type=F32) * factor
        query = query.astype(BF16)
        for pair in range(TILE // PAIR):
            both = query[:, pair * PAIR : (pair + 1) * PAIR]
            at = tile * (TILE // HEAD_DIM) + 2 * pair
            qm[at] = both * left
            qm[at + 1] = both * right

    acc[...] = jnp.zeros_like(acc)
    summed[...] = jnp.zeros_like(summed)
    high[...] = jnp.full_like(high, 2 * LOW)
    ones = jnp.ones((16, rows), BF16)

    def attend(owner):
        block = span(owner, rows)

        @pl.loop(0, width // TILE)
        def _(tile):
            key = jnp.dot(
                hid[block, :],
                wp[:, pl.ds(pl.multiple_of(width + tile * TILE, TILE), TILE)],
                preferred_element_type=F32,
            )
            kbuf[:, span(tile, TILE)] = key.astype(BF16)
            value = jnp.dot(
                hid[block, :],
                wp[:, pl.ds(pl.multiple_of(2 * width + tile * TILE, TILE), TILE)],
                preferred_element_type=F32,
            )
            vt[span(tile, TILE), :] = value.T.astype(BF16)

        position = lax.broadcasted_iota(jnp.int32, (rows, PAIR), 0) + owner * rows
        bias[...] = jnp.where(position < length, 0.0, LOW)

        @pl.loop(0, pairs)
        def _(pair):
            key = kbuf[:, span(pair, PAIR)]
            for side in range(2):
                head = 2 * pair + side
                scores = lax.dot_general(
                    key, qm[head], (((1,), (1,)), ((), ())), preferred_element_type=F32
                )
                scores = scores + jnp.concatenate([bias[...]] * (rows // PAIR), axis=1)
                old = high[head, 0:1, :]
                top = jnp.maximum(old, jnp.max(scores, axis=0, keepdims=True))
                expo = jnp.exp2(scores - top).astype(BF16)
                alpha = jnp.exp2(old - top)
                value = jnp.concatenate([vt[span(head, HEAD_DIM), :], ones], axis=0)
                got = jnp.dot(value, expo, preferred_element_type=F32)
                mine = span(head, HEAD_DIM)
                acc[mine, :] = acc[mine, :] * alpha + got[:HEAD_DIM]
                summed[head] = summed[head] * alpha + got[HEAD_DIM : HEAD_DIM + 8]
                high[head] = jnp.broadcast_to(top, (8, rows))

    @pl.loop(0, 2 * seq_size - 1)
    def _(slot):
        step = (slot + 1) // 2
        upper = (slot + 1) % 2
        owner = rank - step + 2 * step * upper

        @pl.when(jnp.logical_and(upper == 0, step >= 1))
        def _():
            for half in range(HALVES):
                for upward in (True, False):

                    @pl.when(holds(upward, step))
                    def _(upward=upward, half=half):
                        chain(upward, step, half, True).wait_recv()

                        @pl.when(has_next(upward))
                        def _():
                            chain(upward, step + 1, half, False).start()

            for index, (stage, piece) in enumerate(events):

                @pl.when(step == min(1 + index, seq_size - 1))
                def _(stage=stage, piece=piece):
                    ups.pass_on(stage, piece)
                    downs.pass_on(stage, piece)

        @pl.when(jnp.logical_and(owner >= 0, owner < seq_size))
        def _():
            attend(owner)

    @pl.loop(0, pairs)
    def _(pair):
        total = acc[span(pair, PAIR), :]
        low_part = total[:HEAD_DIM] / summed[2 * pair, 0:1, :]
        high_part = total[HEAD_DIM:] / summed[2 * pair + 1, 0:1, :]
        att[:, span(pair, PAIR)] = jnp.concatenate([low_part, high_part], axis=0).T.astype(BF16)

    loads[2].wait()

    @pl.loop(0, width // TILE)
    def _(tile):
        here = span(tile, TILE)
        mixed = jnp.dot(att[...], wo[:, here], preferred_element_type=F32)
        outer[:, here] = mixed + hid[own, here].astype(F32)

    few = 64

    @pl.loop(0, rows // few)
    def _(index):
        here = span(index, few)
        normed[here, :] = layer_norm(outer[here, :], gain1[...], shift1[...]).astype(BF16)

    loads[3].wait()
    for piece in range(1 << (bits - 1)):
        ups.pass_on(bits - 1, piece)

    @pl.loop(0, ff // TILE)
    def _(tile):
        here = span(tile, TILE)
        before = jnp.dot(normed[...], up[:, here], preferred_element_type=F32)
        half = 0.5 * before
        inner[:, here] = (half + half * lax.erf(before * math.sqrt(0.5))).astype(BF16)

    loads[4].wait()
    for piece in range(1 << (bits - 1)):
        downs.pass_on(bits - 1, piece)

    @pl.loop(0, width // TILE)
    def _(tile):
        here = span(tile, TILE)
        back_again = lax.dot_general(
            inner[...], down[here, :], (((1,), (1,)), ((), ())), preferred_element_type=F32
        )
        outer[:, here] = back_again + normed[:, here].astype(F32)

    def finish(index, carry):
        here = span(index, few)
        done = layer_norm(outer[here, :], gain2[...], shift2[...])
        final[here, :] = done.astype(BF16)
        position = lax.broadcasted_iota(jnp.int32, (few, 1), 0) + (rank * rows + index * few)
        done = jnp.where(position < length, done, 0.0)
        return carry + jnp.sum(done, axis=0, keepdims=True)

    local_total = lax.fori_loop(0, rows // few, finish, jnp.zeros((1, width), F32))
    write = pltpu.make_async_copy(final, out_hbm.at[0], local_sem.at[0])
    write.start()

    totals[rank] = local_total

    def spread(ref, axis, mine, size, step, sends, recvs, incoming):
        slot = (mine - step + size) % size if incoming else mine
        return pltpu.make_async_remote_copy(
            src_ref=ref.at[slot],
            dst_ref=ref.at[slot],
            send_sem=sends.at[step - 1],
            recv_sem=recvs.at[step - 1],
            device_id={axis: (mine + step) % size},
            device_id_type=MESH,
        )

    for step in range(1, seq_size):
        spread(totals, "seq", rank, seq_size, step, tot_send, tot_recv, False).start()

    asked = query_ref[...]
    asked = asked / jnp.sqrt(jnp.sum(asked * asked, axis=-1, keepdims=True) + 1e-06)
    asked = asked.astype(BF16).astype(F32)

    for step in range(1, seq_size):
        spread(totals, "seq", rank, seq_size, step, tot_send, tot_recv, True).wait_recv()
    pooled = totals[0]
    for place in range(1, seq_size):
        pooled = pooled + totals[place]
    pooled = pooled / length.astype(F32)
    embedding = pooled / jnp.sqrt(jnp.sum(pooled * pooled, axis=-1, keepdims=True) + 1e-06)
    emb_out[...] = embedding
    embeds[group] = embedding
    for step in range(1, grp_size):
        spread(embeds, "grp", group, grp_size, step, emb_send, emb_recv, False).start()

    for step in range(1, seq_size):
        spread(totals, "seq", rank, seq_size, step, tot_send, tot_recv, False).wait_send()
        for half in range(HALVES):
            for upward in (True, False):

                @pl.when(jnp.logical_and(has_next(upward), holds(upward, step - 1)))
                def _(upward=upward, half=half, step=step):
                    chain(upward, step, half, False, step == 1).wait_send()

    ups.drain()
    downs.drain()

    for step in range(1, grp_size):
        spread(embeds, "grp", group, grp_size, step, emb_send, emb_recv, True).wait_recv()
    count = asked.shape[0]
    row = lax.broadcasted_iota(jnp.int32, (count, 1), 0)
    wanted = jnp.zeros((count, 1), jnp.int32)
    for place in range(count):
        wanted = jnp.where(row == place, positive_ref[place], wanted)
    picked = jnp.zeros((count, 1), F32)
    weight = jnp.zeros((count, 1), F32)
    for place in range(grp_size):
        short = embeds[place].astype(BF16).astype(F32)
        logit = 20.0 * jnp.sum(asked * short, axis=-1, keepdims=True)
        picked = picked + jnp.where(wanted == place, logit, 0.0)
        weight = weight + jnp.exp(logit)
    loss_out[...] = jnp.log(weight) - picked
    for step in range(1, grp_size):
        spread(embeds, "grp", group, grp_size, step, emb_send, emb_recv, False).wait_send()
    write.wait()


def body(
    seq_size,
    grp_size,
    hidden_in,
    lengths,
    project_weight,
    output_weight,
    first_gain,
    first_shift,
    up_weight,
    down_weight,
    second_gain,
    second_shift,
    queries,
    positive,
):
    rows, width = hidden_in.shape[1:]
    ff = up_weight.shape[1]
    heads = width // HEAD_DIM
    count = queries.shape[0]
    wide = lambda vector: vector.reshape(1, -1)
    vmem = pl.BlockSpec(memory_space=pltpu.VMEM)
    smem = pl.BlockSpec(memory_space=pltpu.SMEM)
    hbm = pl.BlockSpec(memory_space=pl.ANY)
    dma = pltpu.SemaphoreType.DMA
    chain_sems = [dma(((seq_size - 1) * HALVES,))] * 4
    pieces = [dma((grp_size - 1,))] * 4
    hidden_out, embedding, loss = pl.pallas_call(
        functools.partial(kernel, seq_size, grp_size),
        out_shape=[
            jax.ShapeDtypeStruct(hidden_in.shape, BF16),
            jax.ShapeDtypeStruct((1, width), F32),
            jax.ShapeDtypeStruct((count, 1), F32),
        ],
        in_specs=[hbm, smem, hbm, hbm, vmem, vmem, hbm, hbm, vmem, vmem, vmem, smem],
        out_specs=[hbm, vmem, vmem],
        scratch_shapes=[
            pltpu.VMEM((seq_size * rows, width), BF16),
            pltpu.VMEM((width, 3 * width), BF16),
            pltpu.VMEM((width, width), BF16),
            pltpu.VMEM((width, ff), BF16),
            pltpu.VMEM((width, ff), BF16),
            pltpu.VMEM((heads, rows, PAIR), BF16),
            pltpu.VMEM((rows, width), BF16),
            pltpu.VMEM((width, rows), BF16),
            pltpu.VMEM((width, rows), F32),
            pltpu.VMEM((heads, 8, rows), F32),
            pltpu.VMEM((heads, 8, rows), F32),
            pltpu.VMEM((rows, PAIR), F32),
            pltpu.VMEM((rows, width), BF16),
            pltpu.VMEM((rows, width), BF16),
            pltpu.VMEM((rows, ff), BF16),
            pltpu.VMEM((rows, width), F32),
            pltpu.VMEM((rows, width), BF16),
            pltpu.VMEM((seq_size, 1, width), F32),
            pltpu.VMEM((grp_size, 1, width), F32),
            dma((5,)),
            *chain_sems,
            *pieces,
            dma((seq_size - 1,)),
            dma((seq_size - 1,)),
            dma((grp_size - 1,)),
            dma((grp_size - 1,)),
        ],
        compiler_params=pltpu.CompilerParams(
            collective_id=0, has_side_effects=True, vmem_limit_bytes=67_043_328
        ),
        cost_estimate=pl.CostEstimate(
            flops=8 * rows * width * ff, bytes_accessed=16 * width * ff, transcendentals=rows * ff
        ),
    )(
        hidden_in,
        lengths,
        project_weight,
        output_weight,
        wide(first_gain),
        wide(first_shift),
        up_weight,
        down_weight,
        wide(second_gain),
        wide(second_shift),
        queries,
        positive,
    )
    return hidden_out, embedding, loss.reshape(count)


def solution(mesh):
    in_specs = (
        P("grp", "seq", None),
        P("grp"),
        P(),
        P(),
        P(),
        P(),
        P("grp", None),
        P("grp", None),
        P(),
        P(),
        P("grp", None),
        P("grp"),
    )
    out_specs = (P("grp", "seq", None), P("grp", None), P("grp"))
    sized = functools.partial(body, mesh.shape["seq"], mesh.shape["grp"])
    return jax.shard_map(sized, mesh=mesh, in_specs=in_specs, out_specs=out_specs, check_vma=False)
```

profile of v0, /device:TPU:0, one launch (start us, length us, event | category | flops | bytes accessed | tf_op | source)
XLA Modules:
  0.0 123.5 jit_solution(3223706315263434470)
XLA Ops:
  1.3 117.4 %shard_map.139 = (bf16[1,512,1024]{2,1,0:T(8,128)(2,1)}, f32[1,1024]{1,0:T(1,128)}, f32[8,1]{1,0:T(8,128)}) custom-call(bf16[1,512,1024]{2,1,0:T(8,128)(2,1)} %tok_hbm.1, s32[1]{0:T(128)S(6)} %copy.17.length_ref, bf16[1024,3072]{1,0:T(8,128)(2,1)} %wp_hbm.1, bf16[1024,1024]{1,0:T(8,128)(2,1)} %wo_hbm.1, f32[1,1024]{1,0:T(1,128)} %bitcast.4, ...), custom_call_target="tpu_custom_call" | custom-call | flops 17179869184 | bytes 67108864 | tf_op jit(solution)/shard_map/pallas_call | solution.py:444
  118.7 1.3 %reduce = f32[8]{0:T(128)} reduce(f32[8,1]{1,0:T(8,128)} %get-tuple-element.8, f32[]{:T(128)} %constant.2), dimensions={1}, to_apply=%get-tuple-element.8.reduce_sub_computation | reduce | bytes 68 | tf_op jit(solution)/shard_map/pallas_call | solution.py:444
  120.0 2.3 %copy.18 = bf16[1,512,1024]{2,1,0:T(8,128)(2,1)} copy(bf16[1,512,1024]{2,1,0:T(8,128)(2,1)} %get-tuple-element.12) | data formatting | bytes 2097152
  122.3 1.3 %copy.19 = f32[1,1024]{1,0:T(1,128)} copy(f32[1,1024]{1,0:T(1,128)} %get-tuple-element.13) | data formatting | bytes 8192
where the time goes:
time: 124 us
  Pallas kernels  117 us (94%)
  local copies, waits for them, and re-layouts  3.53 us (3%)
  other arithmetic  1.31 us (1%)
  between operations  1.29 us (1%)
    pallas_call x1, Pallas kernels, body(): pl.pallas_call(functools.partial(kernel, seq_size, grp_size), out_shape=[...  117 us
    unnamed x2, local copies, waits for them, and re-layouts  3.53 us

commit v1 on v0

--- a/solution.py
+++ b/solution.py
@@ -12,7 +12,8 @@
 PAIR = 2 * HEAD_DIM
 LOW = -1e30
 TILE = 256
-HALVES = 2
+HALVES = 4
+STRIPS = 8
 MESH = pl.DeviceIdType.MESH
 F32 = jnp.float32
 BF16 = jnp.bfloat16
@@ -81,16 +82,22 @@
     length_ref,
     wp_hbm,
     wo_hbm,
+    gain1_hbm,
+    shift1_hbm,
+    up_hbm,
+    down_hbm,
+    gain2_hbm,
+    shift2_hbm,
+    query_hbm,
+    positive_ref,
+    out_hbm,
+    emb_hbm,
+    loss_hbm,
     gain1,
     shift1,
-    up_hbm,
-    down_hbm,
     gain2,
     shift2,
     query_ref,
-    positive_ref,
-    out_hbm,
-    emb_out,
     loss_out,
     hid,
     wp,
@@ -104,6 +111,7 @@
     high,
     summed,
     bias,
+    scores,
     att,
     normed,
     inner,
@@ -156,6 +164,11 @@
         pltpu.make_async_copy(wo_hbm, wo, local_sem.at[2]),
         pltpu.make_async_copy(up_hbm, up.at[span(group, up_hbm.shape[0])], local_sem.at[3]),
         pltpu.make_async_copy(down_hbm, down.at[span(group, down_hbm.shape[0])], local_sem.at[4]),
+        pltpu.make_async_copy(gain1_hbm, gain1, local_sem.at[5]),
+        pltpu.make_async_copy(shift1_hbm, shift1, local_sem.at[6]),
+        pltpu.make_async_copy(gain2_hbm, gain2, local_sem.at[7]),
+        pltpu.make_async_copy(shift2_hbm, shift2, local_sem.at[8]),
+        pltpu.make_async_copy(query_hbm, query_ref, local_sem.at[9]),
     ]
     for load in loads:
         load.start()
@@ -197,35 +210,34 @@
         ups.begin(stage)
         downs.begin(stage)
     events = [(stage, piece) for stage in range(bits - 1) for piece in range(1 << stage)]
+    early, late = events[: seq_size - 2], events[seq_size - 2 :]
 
     loads[0].wait()
     loads[1].wait()
 
-    lane = lax.broadcasted_iota(jnp.int32, (1, PAIR), 1)
-    left = jnp.where(lane < HEAD_DIM, 1.0, 0.0).astype(BF16)
-    right = jnp.where(lane < HEAD_DIM, 0.0, 1.0).astype(BF16)
     factor = math.log2(math.e) / math.sqrt(HEAD_DIM)
     own = span(rank, rows)
 
-    @pl.loop(0, width // TILE)
+    @pl.loop(0, width // TILE, unroll=2)
     def _(tile):
         query = jnp.dot(hid[own, :], wp[:, span(tile, TILE)], preferred_element_type=F32) * factor
-        query = query.astype(BF16)
+        query = query.T.astype(BF16)
         for pair in range(TILE // PAIR):
-            both = query[:, pair * PAIR : (pair + 1) * PAIR]
             at = tile * (TILE // HEAD_DIM) + 2 * pair
-            qm[at] = both * left
-            qm[at + 1] = both * right
+            here = pair * PAIR
+            blank = jnp.zeros((HEAD_DIM, rows), BF16)
+            qm[at] = jnp.concatenate([query[here : here + HEAD_DIM], blank], axis=0)
+            qm[at + 1] = jnp.concatenate([blank, query[here + HEAD_DIM : here + PAIR]], axis=0)
 
     acc[...] = jnp.zeros_like(acc)
     summed[...] = jnp.zeros_like(summed)
     high[...] = jnp.full_like(high, 2 * LOW)
-    ones = jnp.ones((16, rows), BF16)
-
-    def attend(owner):
-        block = span(owner, rows)
-
-        @pl.loop(0, width // TILE)
+    ones = jnp.ones((16, part), BF16)
+
+    def attend(unit):
+        block = span(unit, part)
+
+        @pl.loop(0, width // TILE, unroll=2)
         def _(tile):
             key = jnp.dot(
                 hid[block, :],
@@ -240,77 +252,91 @@
             )
             vt[span(tile, TILE), :] = value.T.astype(BF16)
 
-        position = lax.broadcasted_iota(jnp.int32, (rows, PAIR), 0) + owner * rows
+        position = lax.broadcasted_iota(jnp.int32, (part, PAIR), 0) + unit * part
         bias[...] = jnp.where(position < length, 0.0, LOW)
 
-        @pl.loop(0, pairs)
-        def _(pair):
-            key = kbuf[:, span(pair, PAIR)]
+        def score(pair, place):
+            key = kbuf[:, pl.ds(pair * PAIR, PAIR)]
+            shift = jnp.concatenate([bias[...]] * (rows // PAIR), axis=1)
+            for side in range(2):
+                scores[place, side] = shift + jnp.dot(
+                    key, qm[2 * pair + side], preferred_element_type=F32
+                )
+
+        def weigh(pair, place):
             for side in range(2):
                 head = 2 * pair + side
-                scores = lax.dot_general(
-                    key, qm[head], (((1,), (1,)), ((), ())), preferred_element_type=F32
-                )
-                scores = scores + jnp.concatenate([bias[...]] * (rows // PAIR), axis=1)
+                score_now = scores[place, side]
                 old = high[head, 0:1, :]
-                top = jnp.maximum(old, jnp.max(scores, axis=0, keepdims=True))
-                expo = jnp.exp2(scores - top).astype(BF16)
+                top = jnp.maximum(old, jnp.max(score_now, axis=0, keepdims=True))
+                expo = jnp.exp2(score_now - top).astype(BF16)
                 alpha = jnp.exp2(old - top)
-                value = jnp.concatenate([vt[span(head, HEAD_DIM), :], ones], axis=0)
+                value = jnp.concatenate([vt[pl.ds(head * HEAD_DIM, HEAD_DIM), :], ones], axis=0)
                 got = jnp.dot(value, expo, preferred_element_type=F32)
-                mine = span(head, HEAD_DIM)
+                mine = pl.ds(head * HEAD_DIM, HEAD_DIM)
                 acc[mine, :] = acc[mine, :] * alpha + got[:HEAD_DIM]
                 summed[head] = summed[head] * alpha + got[HEAD_DIM : HEAD_DIM + 8]
                 high[head] = jnp.broadcast_to(top, (8, rows))
 
-    @pl.loop(0, 2 * seq_size - 1)
+        score(0, 0)
+        for pair in range(pairs):
+            if pair + 1 < pairs:
+                score(pair + 1, (pair + 1) % 2)
+            weigh(pair, pair % 2)
+
+    @pl.loop(0, seq_size * HALVES)
     def _(slot):
-        step = (slot + 1) // 2
-        upper = (slot + 1) % 2
-        owner = rank - step + 2 * step * upper
-
-        @pl.when(jnp.logical_and(upper == 0, step >= 1))
-        def _():
-            for half in range(HALVES):
-                for upward in (True, False):
-
-                    @pl.when(holds(upward, step))
-                    def _(upward=upward, half=half):
-                        chain(upward, step, half, True).wait_recv()
-
-                        @pl.when(has_next(upward))
-                        def _():
-                            chain(upward, step + 1, half, False).start()
-
-            for index, (stage, piece) in enumerate(events):
-
-                @pl.when(step == min(1 + index, seq_size - 1))
-                def _(stage=stage, piece=piece):
-                    ups.pass_on(stage, piece)
-                    downs.pass_on(stage, piece)
-
-        @pl.when(jnp.logical_and(owner >= 0, owner < seq_size))
-        def _():
-            attend(owner)
-
-    @pl.loop(0, pairs)
+        step = slot // HALVES
+        half = slot % HALVES
+        for upward in (True, False):
+
+            @pl.when(jnp.logical_and(step >= 1, holds(upward, step)))
+            def _(upward=upward):
+                chain(upward, step, half, True).wait_recv()
+
+                @pl.when(has_next(upward))
+                def _():
+                    chain(upward, step + 1, half, False).start()
+
+        for index, (stage, piece) in enumerate(early):
+
+            @pl.when(slot == (2 + index) * HALVES - 1)
+            def _(stage=stage, piece=piece):
+                ups.pass_on(stage, piece)
+                downs.pass_on(stage, piece)
+
+        @pl.loop(0, 2)
+        def _(upper):
+            owner = rank - step + 2 * step * upper
+
+            @pl.when((owner >= 0) & (owner < seq_size) & (step + upper >= 1))
+            def _():
+                attend(owner * HALVES + half)
+
+    for stage, piece in late:
+        ups.pass_on(stage, piece)
+        downs.pass_on(stage, piece)
+
+    @pl.loop(0, pairs, unroll=4)
     def _(pair):
         total = acc[span(pair, PAIR), :]
-        low_part = total[:HEAD_DIM] / summed[2 * pair, 0:1, :]
-        high_part = total[HEAD_DIM:] / summed[2 * pair + 1, 0:1, :]
+        low_part = total[:HEAD_DIM] * (1.0 / summed[2 * pair, 0:1, :])
+        high_part = total[HEAD_DIM:] * (1.0 / summed[2 * pair + 1, 0:1, :])
         att[:, span(pair, PAIR)] = jnp.concatenate([low_part, high_part], axis=0).T.astype(BF16)
 
     loads[2].wait()
 
-    @pl.loop(0, width // TILE)
+    @pl.loop(0, width // TILE, unroll=2)
     def _(tile):
         here = span(tile, TILE)
         mixed = jnp.dot(att[...], wo[:, here], preferred_element_type=F32)
         outer[:, here] = mixed + hid[own, here].astype(F32)
 
-    few = 64
-
-    @pl.loop(0, rows // few)
+    for load in loads[5:]:
+        load.wait()
+    few = 128
+
+    @pl.loop(0, rows // few, unroll=2)
     def _(index):
         here = span(index, few)
         normed[here, :] = layer_norm(outer[here, :], gain1[...], shift1[...]).astype(BF16)
@@ -319,7 +345,7 @@
     for piece in range(1 << (bits - 1)):
         ups.pass_on(bits - 1, piece)
 
-    @pl.loop(0, ff // TILE)
+    @pl.loop(0, ff // TILE, unroll=4)
     def _(tile):
         here = span(tile, TILE)
         before = jnp.dot(normed[...], up[:, here], preferred_element_type=F32)
@@ -330,7 +356,7 @@
     for piece in range(1 << (bits - 1)):
         downs.pass_on(bits - 1, piece)
 
-    @pl.loop(0, width // TILE)
+    @pl.loop(0, width // TILE, unroll=2)
     def _(tile):
         here = span(tile, TILE)
         back_again = lax.dot_general(
@@ -346,7 +372,9 @@
         done = jnp.where(position < length, done, 0.0)
         return carry + jnp.sum(done, axis=0, keepdims=True)
 
-    local_total = lax.fori_loop(0, rows // few, finish, jnp.zeros((1, width), F32))
+    local_total = lax.fori_loop(
+        0, rows // few, finish, jnp.zeros((1, width), F32), unroll=2
+    )
     write = pltpu.make_async_copy(final, out_hbm.at[0], local_sem.at[0])
     write.start()
 
@@ -377,8 +405,9 @@
         pooled = pooled + totals[place]
     pooled = pooled / length.astype(F32)
     embedding = pooled / jnp.sqrt(jnp.sum(pooled * pooled, axis=-1, keepdims=True) + 1e-06)
-    emb_out[...] = embedding
     embeds[group] = embedding
+    keep = pltpu.make_async_copy(embeds.at[group], emb_hbm, local_sem.at[1])
+    keep.start()
     for step in range(1, grp_size):
         spread(embeds, "grp", group, grp_size, step, emb_send, emb_recv, False).start()
 
@@ -408,10 +437,32 @@
         logit = 20.0 * jnp.sum(asked * short, axis=-1, keepdims=True)
         picked = picked + jnp.where(wanted == place, logit, 0.0)
         weight = weight + jnp.exp(logit)
-    loss_out[...] = jnp.log(weight) - picked
+    loss = jnp.log(weight) - picked
+    loss_out[...] = jnp.broadcast_to(loss, (count, PAIR)).T[0:1, :]
+    give = pltpu.make_async_copy(loss_out, loss_hbm, local_sem.at[2])
+    give.start()
     for step in range(1, grp_size):
         spread(embeds, "grp", group, grp_size, step, emb_send, emb_recv, False).wait_send()
     write.wait()
+    keep.wait()
+    give.wait()
+
+
+def hand_over(hidden, embedding, loss, hidden_out, embedding_out, loss_out, *held):
+    strips, small, short, come, go = held
+    strip = strips.shape[0] // STRIPS
+    at = lambda index: pl.ds(index * strip, strip)
+    legs = [(hidden.at[0, at(i)], strips.at[at(i)], hidden_out.at[0, at(i)]) for i in range(STRIPS)]
+    legs += [(embedding, small, embedding_out), (loss, short, loss_out)]
+    comes = [pltpu.make_async_copy(leg[0], leg[1], come.at[i]) for i, leg in enumerate(legs)]
+    goes = [pltpu.make_async_copy(leg[1], leg[2], go.at[i]) for i, leg in enumerate(legs)]
+    for copy in comes:
+        copy.start()
+    for index in range(len(legs)):
+        comes[index].wait()
+        goes[index].start()
+    for copy in goes:
+        copy.wait()
 
 
 def body(
@@ -435,7 +486,6 @@
     heads = width // HEAD_DIM
     count = queries.shape[0]
     wide = lambda vector: vector.reshape(1, -1)
-    vmem = pl.BlockSpec(memory_space=pltpu.VMEM)
     smem = pl.BlockSpec(memory_space=pltpu.SMEM)
     hbm = pl.BlockSpec(memory_space=pl.ANY)
     dma = pltpu.SemaphoreType.DMA
@@ -446,23 +496,27 @@
         out_shape=[
             jax.ShapeDtypeStruct(hidden_in.shape, BF16),
             jax.ShapeDtypeStruct((1, width), F32),
-            jax.ShapeDtypeStruct((count, 1), F32),
+            jax.ShapeDtypeStruct((1, count), F32),
         ],
-        in_specs=[hbm, smem, hbm, hbm, vmem, vmem, hbm, hbm, vmem, vmem, vmem, smem],
-        out_specs=[hbm, vmem, vmem],
+        in_specs=[hbm, smem, hbm, hbm, hbm, hbm, hbm, hbm, hbm, hbm, hbm, smem],
+        out_specs=[hbm, hbm, hbm],
         scratch_shapes=[
+            *[pltpu.VMEM((1, width), F32)] * 4,
+            pltpu.VMEM((count, width), F32),
+            pltpu.VMEM((1, count), F32),
             pltpu.VMEM((seq_size * rows, width), BF16),
             pltpu.VMEM((width, 3 * width), BF16),
             pltpu.VMEM((width, width), BF16),
             pltpu.VMEM((width, ff), BF16),
             pltpu.VMEM((width, ff), BF16),
-            pltpu.VMEM((heads, rows, PAIR), BF16),
-            pltpu.VMEM((rows, width), BF16),
-            pltpu.VMEM((width, rows), BF16),
+            pltpu.VMEM((heads, PAIR, rows), BF16),
+            pltpu.VMEM((rows // HALVES, width), BF16),
+            pltpu.VMEM((width, rows // HALVES), BF16),
             pltpu.VMEM((width, rows), F32),
             pltpu.VMEM((heads, 8, rows), F32),
             pltpu.VMEM((heads, 8, rows), F32),
-            pltpu.VMEM((rows, PAIR), F32),
+            pltpu.VMEM((rows // HALVES, PAIR), F32),
+            pltpu.VMEM((2, 2, rows // HALVES, rows), F32),
             pltpu.VMEM((rows, width), BF16),
             pltpu.VMEM((rows, width), BF16),
             pltpu.VMEM((rows, ff), BF16),
@@ -470,7 +524,7 @@
             pltpu.VMEM((rows, width), BF16),
             pltpu.VMEM((seq_size, 1, width), F32),
             pltpu.VMEM((grp_size, 1, width), F32),
-            dma((5,)),
+            dma((10,)),
             *chain_sems,
             *pieces,
             dma((seq_size - 1,)),
@@ -479,7 +533,7 @@
             dma((grp_size - 1,)),
         ],
         compiler_params=pltpu.CompilerParams(
-            collective_id=0, has_side_effects=True, vmem_limit_bytes=67_043_328
+            collective_id=0, has_side_effects=True, vmem_limit_bytes=54 << 20
         ),
         cost_estimate=pl.CostEstimate(
             flops=8 * rows * width * ff, bytes_accessed=16 * width * ff, transcendentals=rows * ff
@@ -498,6 +552,26 @@
         queries,
         positive,
     )
+    hidden_out, embedding, loss = pl.pallas_call(
+        hand_over,
+        out_shape=[
+            jax.ShapeDtypeStruct(hidden_out.shape, BF16),
+            jax.ShapeDtypeStruct(embedding.shape, F32),
+            jax.ShapeDtypeStruct(loss.shape, F32),
+        ],
+        in_specs=[hbm, hbm, hbm],
+        out_specs=[hbm, hbm, hbm],
+        scratch_shapes=[
+            pltpu.VMEM((rows, width), BF16),
+            pltpu.VMEM(embedding.shape, F32),
+            pltpu.VMEM(loss.shape, F32),
+            dma((STRIPS + 2,)),
+            dma((STRIPS + 2,)),
+        ],
+        cost_estimate=pl.CostEstimate(
+            flops=rows * width, bytes_accessed=4 * rows * width, transcendentals=0
+        ),
+    )(hidden_out, embedding, loss)
     return hidden_out, embedding, loss.reshape(count)
 
 

time: 124 us -> 104 us (0.84)
  Pallas kernels: 117 us -> 103 us
  local copies, waits for them, and re-layouts: 3.53 us -> 0 us
  other arithmetic: 1.31 us -> 0 us
    pallas_call x1, Pallas kernels: 117 us -> 100 us  [body(): pl.pallas_call(functools.partial(kernel, seq_size, grp_size), out_shape=[...]
    unnamed x2 -> x0, local copies, waits for them, and re-layouts: 3.53 us -> none
    pallas_call x0 -> x1, Pallas kernels: none -> 2.13 us  [body(): pl.pallas_call(hand_over, out_shape=[jax.ShapeDtypeStruct(hidden_out.shap...]
    pallas_call x1 -> x0, other arithmetic: 1.31 us -> none  [body(): pl.pallas_call(functools.partial(kernel, seq_size, grp_size), out_shape=[...]
where the time goes in v1:
time: 104 us
  Pallas kernels  103 us (99%)
  between operations  1.29 us (1%)
    pallas_call x1, Pallas kernels, body(): pl.pallas_call(functools.partial(kernel, seq_size, grp_size), out_shape=[...  100 us
    pallas_call x1, Pallas kernels, body(): pl.pallas_call(hand_over, out_shape=[jax.ShapeDtypeStruct(hidden_out.shap...  2.13 us

profile of v1, /device:TPU:0, one launch (start us, length us, event | category | flops | bytes accessed | tf_op | source)
XLA Modules:
  0.0 103.9 jit_solution(17723381094295387405)
XLA Ops:
  1.3 100.5 %shard_map.139 = (bf16[1,512,1024]{2,1,0:T(8,128)(2,1)}, f32[1,1024]{1,0:T(1,128)}, f32[1,8]{1,0:T(1,128)}) custom-call(bf16[1,512,1024]{2,1,0:T(8,128)(2,1)} %tok_hbm.1, s32[1]{0:T(128)S(6)} %copy.15.length_ref, bf16[1024,3072]{1,0:T(8,128)(2,1)} %wp_hbm.1, bf16[1024,1024]{1,0:T(8,128)(2,1)} %wo_hbm.1, f32[1,1024]{1,0:T(1,128)} %bitcast.5, ...), custom_call_target="tpu_custom_call" | custom-call | flops 17179869184 | bytes 67108864 | tf_op jit(solution)/shard_map/pallas_call | solution.py:494
  101.7 2.1 %shard_map.140 = (bf16[1,512,1024]{2,1,0:T(8,128)(2,1)}, f32[1,1024]{1,0:T(1,128)}, f32[1,8]{1,0:T(1,128)}) custom-call(bf16[1,512,1024]{2,1,0:T(8,128)(2,1)} %get-tuple-element.9.hidden, f32[1,1024]{1,0:T(1,128)} %get-tuple-element.10.embedding, f32[1,8]{1,0:T(1,128)} %get-tuple-element.11.loss), custom_call_target="tpu_custom_call" | custom-call | flops 524288 | bytes 2097152 | tf_op jit(solution)/shard_map/pallas_call | solution.py:555

commit v2 on v1

--- a/solution.py
+++ b/solution.py
@@ -12,6 +12,7 @@
 PAIR = 2 * HEAD_DIM
 LOW = -1e30
 TILE = 256
+WIDE = 512
 HALVES = 4
 STRIPS = 8
 MESH = pl.DeviceIdType.MESH
@@ -88,17 +89,12 @@
     down_hbm,
     gain2_hbm,
     shift2_hbm,
-    query_hbm,
-    positive_ref,
     out_hbm,
-    emb_hbm,
-    loss_hbm,
+    table_hbm,
     gain1,
     shift1,
     gain2,
     shift2,
-    query_ref,
-    loss_out,
     hid,
     wp,
     wo,
@@ -168,10 +164,7 @@
         pltpu.make_async_copy(shift1_hbm, shift1, local_sem.at[6]),
         pltpu.make_async_copy(gain2_hbm, gain2, local_sem.at[7]),
         pltpu.make_async_copy(shift2_hbm, shift2, local_sem.at[8]),
-        pltpu.make_async_copy(query_hbm, query_ref, local_sem.at[9]),
     ]
-    for load in loads:
-        load.start()
     pl.semaphore_wait(barrier, seq_size - 1 + grp_size - 1)
 
     def chain(upward, step, half, incoming, first=False):
@@ -202,6 +195,8 @@
             def _(upward=upward, half=half):
                 chain(upward, 1, half, False, True).start()
 
+    for load in loads[:2]:
+        load.start()
     order = list(range(1, bits)) + [0]
     back = list(reversed(range(1, bits))) + [0]
     ups = Gather(up_hbm, up, up_send, up_recv, group, order)
@@ -209,6 +204,8 @@
     for stage in range(bits):
         ups.begin(stage)
         downs.begin(stage)
+    for load in loads[2:]:
+        load.start()
     events = [(stage, piece) for stage in range(bits - 1) for piece in range(1 << stage)]
     early, late = events[: seq_size - 2], events[seq_size - 2 :]
 
@@ -326,9 +323,9 @@
 
     loads[2].wait()
 
-    @pl.loop(0, width // TILE, unroll=2)
+    @pl.loop(0, width // WIDE, unroll=2)
     def _(tile):
-        here = span(tile, TILE)
+        here = span(tile, WIDE)
         mixed = jnp.dot(att[...], wo[:, here], preferred_element_type=F32)
         outer[:, here] = mixed + hid[own, here].astype(F32)
 
@@ -345,9 +342,9 @@
     for piece in range(1 << (bits - 1)):
         ups.pass_on(bits - 1, piece)
 
-    @pl.loop(0, ff // TILE, unroll=4)
+    @pl.loop(0, ff // WIDE, unroll=4)
     def _(tile):
-        here = span(tile, TILE)
+        here = span(tile, WIDE)
         before = jnp.dot(normed[...], up[:, here], preferred_element_type=F32)
         half = 0.5 * before
         inner[:, here] = (half + half * lax.erf(before * math.sqrt(0.5))).astype(BF16)
@@ -356,9 +353,9 @@
     for piece in range(1 << (bits - 1)):
         downs.pass_on(bits - 1, piece)
 
-    @pl.loop(0, width // TILE, unroll=2)
+    @pl.loop(0, width // WIDE, unroll=2)
     def _(tile):
-        here = span(tile, TILE)
+        here = span(tile, WIDE)
         back_again = lax.dot_general(
             inner[...], down[here, :], (((1,), (1,)), ((), ())), preferred_element_type=F32
         )
@@ -376,8 +373,6 @@
         0, rows // few, finish, jnp.zeros((1, width), F32), unroll=2
     )
     write = pltpu.make_async_copy(final, out_hbm.at[0], local_sem.at[0])
-    write.start()
-
     totals[rank] = local_total
 
     def spread(ref, axis, mine, size, step, sends, recvs, incoming):
@@ -393,10 +388,7 @@
 
     for step in range(1, seq_size):
         spread(totals, "seq", rank, seq_size, step, tot_send, tot_recv, False).start()
-
-    asked = query_ref[...]
-    asked = asked / jnp.sqrt(jnp.sum(asked * asked, axis=-1, keepdims=True) + 1e-06)
-    asked = asked.astype(BF16).astype(F32)
+    write.start()
 
     for step in range(1, seq_size):
         spread(totals, "seq", rank, seq_size, step, tot_send, tot_recv, True).wait_recv()
@@ -406,8 +398,6 @@
     pooled = pooled / length.astype(F32)
     embedding = pooled / jnp.sqrt(jnp.sum(pooled * pooled, axis=-1, keepdims=True) + 1e-06)
     embeds[group] = embedding
-    keep = pltpu.make_async_copy(embeds.at[group], emb_hbm, local_sem.at[1])
-    keep.start()
     for step in range(1, grp_size):
         spread(embeds, "grp", group, grp_size, step, emb_send, emb_recv, False).start()
 
@@ -425,6 +415,36 @@
 
     for step in range(1, grp_size):
         spread(embeds, "grp", group, grp_size, step, emb_send, emb_recv, True).wait_recv()
+    keep = pltpu.make_async_copy(embeds, table_hbm, local_sem.at[1])
+    keep.start()
+    for step in range(1, grp_size):
+        spread(embeds, "grp", group, grp_size, step, emb_send, emb_recv, False).wait_send()
+    write.wait()
+    keep.wait()
+
+
+def hand_over(hidden, table_hbm, query_hbm, positive_ref, hidden_out, emb_out, loss_out, *held):
+    strips, table, asked_ref, short, come, go = held
+    strip = strips.shape[0] // STRIPS
+    at = lambda index: pl.ds(index * strip, strip)
+    group = lax.axis_index("grp")
+    legs = [(table_hbm, table), (query_hbm, asked_ref)]
+    legs += [(hidden.at[0, at(i)], strips.at[at(i)]) for i in range(STRIPS)]
+    comes = [pltpu.make_async_copy(*leg, come.at[i]) for i, leg in enumerate(legs)]
+    goes = [(table.at[group], emb_out), (short, loss_out)]
+    goes += [(strips.at[at(i)], hidden_out.at[0, at(i)]) for i in range(STRIPS)]
+    goes = [pltpu.make_async_copy(*leg, go.at[i]) for i, leg in enumerate(goes)]
+    for copy in comes:
+        copy.start()
+    comes[0].wait()
+    comes[1].wait()
+    goes[0].start()
+    for index in range(STRIPS):
+        comes[2 + index].wait()
+        goes[2 + index].start()
+    asked = asked_ref[...]
+    asked = asked / jnp.sqrt(jnp.sum(asked * asked, axis=-1, keepdims=True) + 1e-06)
+    asked = asked.astype(BF16).astype(F32)
     count = asked.shape[0]
     row = lax.broadcasted_iota(jnp.int32, (count, 1), 0)
     wanted = jnp.zeros((count, 1), jnp.int32)
@@ -432,35 +452,14 @@
         wanted = jnp.where(row == place, positive_ref[place], wanted)
     picked = jnp.zeros((count, 1), F32)
     weight = jnp.zeros((count, 1), F32)
-    for place in range(grp_size):
-        short = embeds[place].astype(BF16).astype(F32)
-        logit = 20.0 * jnp.sum(asked * short, axis=-1, keepdims=True)
+    for place in range(table.shape[0]):
+        passage = table[place].astype(BF16).astype(F32)
+        logit = 20.0 * jnp.sum(asked * passage, axis=-1, keepdims=True)
         picked = picked + jnp.where(wanted == place, logit, 0.0)
         weight = weight + jnp.exp(logit)
     loss = jnp.log(weight) - picked
-    loss_out[...] = jnp.broadcast_to(loss, (count, PAIR)).T[0:1, :]
-    give = pltpu.make_async_copy(loss_out, loss_hbm, local_sem.at[2])
-    give.start()
-    for step in range(1, grp_size):
-        spread(embeds, "grp", group, grp_size, step, emb_send, emb_recv, False).wait_send()
-    write.wait()
-    keep.wait()
-    give.wait()
-
-
-def hand_over(hidden, embedding, loss, hidden_out, embedding_out, loss_out, *held):
-    strips, small, short, come, go = held
-    strip = strips.shape[0] // STRIPS
-    at = lambda index: pl.ds(index * strip, strip)
-    legs = [(hidden.at[0, at(i)], strips.at[at(i)], hidden_out.at[0, at(i)]) for i in range(STRIPS)]
-    legs += [(embedding, small, embedding_out), (loss, short, loss_out)]
-    comes = [pltpu.make_async_copy(leg[0], leg[1], come.at[i]) for i, leg in enumerate(legs)]
-    goes = [pltpu.make_async_copy(leg[1], leg[2], go.at[i]) for i, leg in enumerate(legs)]
-    for copy in comes:
-        copy.start()
-    for index in range(len(legs)):
-        comes[index].wait()
-        goes[index].start()
+    short[...] = jnp.broadcast_to(loss, (count, PAIR)).T[0:1, :]
+    goes[1].start()
     for copy in goes:
         copy.wait()
 
@@ -491,19 +490,16 @@
     dma = pltpu.SemaphoreType.DMA
     chain_sems = [dma(((seq_size - 1) * HALVES,))] * 4
     pieces = [dma((grp_size - 1,))] * 4
-    hidden_out, embedding, loss = pl.pallas_call(
+    hidden_out, table = pl.pallas_call(
         functools.partial(kernel, seq_size, grp_size),
         out_shape=[
             jax.ShapeDtypeStruct(hidden_in.shape, BF16),
-            jax.ShapeDtypeStruct((1, width), F32),
-            jax.ShapeDtypeStruct((1, count), F32),
+            jax.ShapeDtypeStruct((grp_size, 1, width), F32),
         ],
-        in_specs=[hbm, smem, hbm, hbm, hbm, hbm, hbm, hbm, hbm, hbm, hbm, smem],
-        out_specs=[hbm, hbm, hbm],
+        in_specs=[hbm, smem, hbm, hbm, hbm, hbm, hbm, hbm, hbm, hbm],
+        out_specs=[hbm, hbm],
         scratch_shapes=[
             *[pltpu.VMEM((1, width), F32)] * 4,
-            pltpu.VMEM((count, width), F32),
-            pltpu.VMEM((1, count), F32),
             pltpu.VMEM((seq_size * rows, width), BF16),
             pltpu.VMEM((width, 3 * width), BF16),
             pltpu.VMEM((width, width), BF16),
@@ -524,7 +520,7 @@
             pltpu.VMEM((rows, width), BF16),
             pltpu.VMEM((seq_size, 1, width), F32),
             pltpu.VMEM((grp_size, 1, width), F32),
-            dma((10,)),
+            dma((9,)),
             *chain_sems,
             *pieces,
             dma((seq_size - 1,)),
@@ -549,29 +545,28 @@
         down_weight,
         wide(second_gain),
         wide(second_shift),
-        queries,
-        positive,
     )
     hidden_out, embedding, loss = pl.pallas_call(
         hand_over,
         out_shape=[
             jax.ShapeDtypeStruct(hidden_out.shape, BF16),
-            jax.ShapeDtypeStruct(embedding.shape, F32),
-            jax.ShapeDtypeStruct(loss.shape, F32),
+            jax.ShapeDtypeStruct((1, width), F32),
+            jax.ShapeDtypeStruct((1, count), F32),
         ],
-        in_specs=[hbm, hbm, hbm],
+        in_specs=[hbm, hbm, hbm, smem],
         out_specs=[hbm, hbm, hbm],
         scratch_shapes=[
             pltpu.VMEM((rows, width), BF16),
-            pltpu.VMEM(embedding.shape, F32),
-            pltpu.VMEM(loss.shape, F32),
+            pltpu.VMEM(table.shape, F32),
+            pltpu.VMEM((count, width), F32),
+            pltpu.VMEM((1, count), F32),
             dma((STRIPS + 2,)),
             dma((STRIPS + 2,)),
         ],
         cost_estimate=pl.CostEstimate(
             flops=rows * width, bytes_accessed=4 * rows * width, transcendentals=0
         ),
-    )(hidden_out, embedding, loss)
+    )(hidden_out, table, queries, positive)
     return hidden_out, embedding, loss.reshape(count)
 
 

time: 104 us -> 103 us (level)
  Pallas kernels: 103 us -> 101 us
    pallas_call x1, Pallas kernels: 100 us -> 98.3 us  [body(): pl.pallas_call(functools.partial(kernel, seq_size, grp_size), out_shape=[...]
where the time goes in v2:
time: 103 us
  Pallas kernels  101 us (98%)
  between operations  1.29 us (1%)
    pallas_call x1, Pallas kernels, body(): pl.pallas_call(functools.partial(kernel, seq_size, grp_size), out_shape=[...  98.3 us
    pallas_call x1, Pallas kernels, body(): pl.pallas_call(hand_over, out_shape=[jax.ShapeDtypeStruct(hidden_out.shap...  2.96 us

profile of v2, /device:TPU:0, one launch (start us, length us, event | category | flops | bytes accessed | tf_op | source)
XLA Modules:
  0.0 102.5 jit_solution(14177144269558251451)
XLA Ops:
  1.3 98.3 %shard_map.139 = (bf16[1,512,1024]{2,1,0:T(8,128)(2,1)}, f32[8,1,1024]{2,1,0:T(1,128)}) custom-call(bf16[1,512,1024]{2,1,0:T(8,128)(2,1)} %tok_hbm.1, s32[1]{0:T(128)S(6)} %copy.15.length_ref, bf16[1024,3072]{1,0:T(8,128)(2,1)} %wp_hbm.1, bf16[1024,1024]{1,0:T(8,128)(2,1)} %wo_hbm.1, f32[1,1024]{1,0:T(1,128)} %bitcast.5, f32[1,1024]{1,0:T(1,128)} %bitcast.6, ...), custom_call_target="tpu_custom_call" | custom-call | flops 17179869184 | bytes 67108864 | tf_op jit(solution)/shard_map/pallas_call | solution.py:493
  99.6 3.0 %shard_map.140 = (bf16[1,512,1024]{2,1,0:T(8,128)(2,1)}, f32[1,1024]{1,0:T(1,128)}, f32[1,8]{1,0:T(1,128)}) custom-call(bf16[1,512,1024]{2,1,0:T(8,128)(2,1)} %get-tuple-element.8.hidden, f32[8,1,1024]{2,1,0:T(1,128)} %get-tuple-element.9.table_hbm, f32[8,1024]{1,0:T(8,128)} %query_hbm.1, s32[8]{0:T(128)} %positive_ref.1), custom_call_target="tpu_custom_call" | custom-call | flops 524288 | bytes 2097152 | tf_op jit(solution)/shard_map/pallas_call | solution.py:549

commit v3 on v2

--- a/solution.py
+++ b/solution.py
@@ -333,7 +333,7 @@
         load.wait()
     few = 128
 
-    @pl.loop(0, rows // few, unroll=2)
+    @pl.loop(0, rows // few, unroll=4)
     def _(index):
         here = span(index, few)
         normed[here, :] = layer_norm(outer[here, :], gain1[...], shift1[...]).astype(BF16)
@@ -370,7 +370,7 @@
         return carry + jnp.sum(done, axis=0, keepdims=True)
 
     local_total = lax.fori_loop(
-        0, rows // few, finish, jnp.zeros((1, width), F32), unroll=2
+        0, rows // few, finish, jnp.zeros((1, width), F32), unroll=4
     )
     write = pltpu.make_async_copy(final, out_hbm.at[0], local_sem.at[0])
     totals[rank] = local_total

time: 103 us -> 102 us (level)
  no operation moved by 1% of the time
where the time goes in v3:
time: 102 us
  Pallas kernels  101 us (99%)
  between operations  1.29 us (1%)
    pallas_call x1, Pallas kernels, body(): pl.pallas_call(functools.partial(kernel, seq_size, grp_size), out_shape=[...  98 us
    pallas_call x1, Pallas kernels, body(): pl.pallas_call(hand_over, out_shape=[jax.ShapeDtypeStruct(hidden_out.shap...  2.96 us

profile of v3, /device:TPU:0, one launch (start us, length us, event | category | flops | bytes accessed | tf_op | source)
XLA Modules:
  0.0 102.2 jit_solution(16260639557836240051)
XLA Ops:
  1.3 98.0 %shard_map.139 = (bf16[1,512,1024]{2,1,0:T(8,128)(2,1)}, f32[8,1,1024]{2,1,0:T(1,128)}) custom-call(bf16[1,512,1024]{2,1,0:T(8,128)(2,1)} %tok_hbm.1, s32[1]{0:T(128)S(6)} %copy.15.length_ref, bf16[1024,3072]{1,0:T(8,128)(2,1)} %wp_hbm.1, bf16[1024,1024]{1,0:T(8,128)(2,1)} %wo_hbm.1, f32[1,1024]{1,0:T(1,128)} %bitcast.5, f32[1,1024]{1,0:T(1,128)} %bitcast.6, ...), custom_call_target="tpu_custom_call" | custom-call | flops 17179869184 | bytes 67108864 | tf_op jit(solution)/shard_map/pallas_call | solution.py:493
  99.3 3.0 %shard_map.140 = (bf16[1,512,1024]{2,1,0:T(8,128)(2,1)}, f32[1,1024]{1,0:T(1,128)}, f32[1,8]{1,0:T(1,128)}) custom-call(bf16[1,512,1024]{2,1,0:T(8,128)(2,1)} %get-tuple-element.8.hidden, f32[8,1,1024]{2,1,0:T(1,128)} %get-tuple-element.9.table_hbm, f32[8,1024]{1,0:T(8,128)} %query_hbm.1, s32[8]{0:T(128)} %positive_ref.1), custom_call_target="tpu_custom_call" | custom-call | flops 524288 | bytes 2097152 | tf_op jit(solution)/shard_map/pallas_call | solution.py:549
